TPU v7x, 32 devices: a whole 2x2x4 slice. The times are simulated.
32 devices in a mesh: row: 8 (over y, x, core), col: 4 (over z).
Axes of the slice: x: 2, y: 2, z: 4, core: 2. Of those that a mesh axis runs over, the one named last changes fastest.
Arguments:
- front_tiles: float32 [2, 2048, 2, 1024], P(None, 'row', None, 'col'), may hold values from -6 to 6, as said below
- lead_tiles: int32 [2, 8], P(None, 'row'), may hold values from 0 to 7
- damping: float32 [2, 1024], P(None, 'col'), may hold values from 1.5 to 6
Outputs:
- factor: float32 [2, 2048, 2, 1024], P(None, 'row', None, 'col')
Inputs may be any that keep to these rules, and one draw needn't show every extreme that they name: `front_tiles`: the front's entries. `lead_tiles`: entries of the first 8 tile rows are not read.
All inputs are finite; a program needn't handle non-finite values.
Results may differ from a plain program's by a relative error of at most 0.00005.
Values sent between devices are 32-bit elements; how exact they have to be, the bound alone decides.
No kernel may reach another device: no remote copies, remote signals or barrier semaphores. Data moves between devices by JAX's collectives and lax.ppermute only.
A program may use at most 64 MiB of HBM per device.

v0:
```python
import jax
import jax.numpy as jnp
from jax import lax
from jax.sharding import PartitionSpec as P


def from_root(value, axis, source):
    kept = jnp.where(lax.axis_index(axis) == source, value, 0).astype(value.dtype)
    return lax.psum(kept, axis)


def pick_tile(tiles, tile_rows, wanted):
    chosen = (tile_rows == wanted)[:, None, None]
    return jnp.sum(jnp.where(chosen, tiles, 0.0), axis=0)


def shards(front_tiles, lead_tiles, damping):
    slot_count, tile_size, col_slot_count, _ = front_tiles.shape
    n_row = lax.axis_size("row")
    n_col = lax.axis_size("col")
    row_at = lax.axis_index("row")
    col_at = lax.axis_index("col")
    n_columns = col_slot_count * n_col
    row_tiles = jnp.arange(slot_count, dtype=jnp.int32) * n_row + row_at
    col_tiles = jnp.arange(col_slot_count, dtype=jnp.int32) * n_col + col_at
    leads = jnp.where(row_tiles < n_columns, 0, lead_tiles[:, 0])
    working = front_tiles
    kept_mask = col_tiles[None, :] >= leads[:, None]
    working = jnp.where(kept_mask[:, None, :, None], working, 0.0)
    identity = jnp.eye(tile_size, dtype=jnp.float32)
    on_diagonal = (row_tiles[:, None] == col_tiles[None, :])[:, None, :, None]
    damp_term = identity[None, :, None, :] * damping[None, None, :, :]
    working = working + jnp.where(on_diagonal, damp_term, 0.0)
    for column in range(n_columns):
        owner_col = column % n_col
        col_slot = column // n_col
        column_panel = working[:, :, col_slot, :]
        diag_source = pick_tile(column_panel, row_tiles, column)
        diag_full = from_root(diag_source, "row", column % n_row)
        symmetric = jnp.tril(diag_full) + jnp.tril(diag_full, -1).T
        lower_factor = jnp.linalg.cholesky(symmetric)
        flattened = column_panel.reshape(slot_count * tile_size, tile_size)
        solved = jax.scipy.linalg.solve_triangular(lower_factor, flattened.T, lower=True).T
        solved = solved.reshape(slot_count, tile_size, tile_size)
        below = (row_tiles > column)[:, None, None]
        at_diag = (row_tiles == column)[:, None, None]
        new_panel = jnp.where(below, solved, jnp.where(at_diag, lower_factor[None], 0.0))
        is_owner = col_at == owner_col
        working = working.at[:, :, col_slot, :].set(jnp.where(is_owner, new_panel, column_panel))
        shared = from_root(new_panel, "col", owner_col)
        for target_slot in range(col_slot_count):
            target = col_tiles[target_slot]
            sep_source = pick_tile(shared, row_tiles, target)
            sep_tile = from_root(sep_source, "row", target)

            def apply_all(current):
                product_update = jnp.dot(
                    shared.reshape(slot_count * tile_size, tile_size),
                    sep_tile.T,
                    precision=lax.Precision.HIGHEST,
                    preferred_element_type=jnp.float32,
                )
                return current - product_update.reshape(slot_count, tile_size, tile_size)

            def keep_same(current):
                return current

            updated = lax.cond(target > column, apply_all, keep_same, working[:, :, target_slot, :])
            working = working.at[:, :, target_slot, :].set(updated)
    final_mask = kept_mask & (row_tiles[:, None] >= col_tiles[None, :])
    result = jnp.where(final_mask[:, None, :, None], working, 0.0)
    return result


def solution(mesh):
    in_specs = (P(None, "row", None, "col"), P(None, "row"), P(None, "col"))
    out_specs = P(None, "row", None, "col")
    return jax.shard_map(shards, mesh=mesh, in_specs=in_specs, out_specs=out_specs, check_vma=False)
```

profile of v0, /device:TPU:0, one launch (start us, length us, event | category | flops | bytes accessed | tf_op | source)
XLA Modules:
  0.0 1757.5 jit_solution(1839295650670124243)
XLA Ops:
  9.5 57.1 %all-reduce.34.cloned.1.call-done = f32[256,256]{1,0:T(8,128)} async-done(((f32[256,256]{1,0:T(8,128)}), f32[256,256]{1,0:T(8,128)}) %all-reduce.34.cloned.1.call-update) | async-done | bytes 262160 | tf_op jit(solution)/shard_map/psum | solution.py:9
  68.2 11.7 cholesky.382
  80.0 9.8 custom-call.25
  90.4 11.7 cholesky.399
  104.4 4.6 while.40
  109.0 19.7 %custom-call.26 = f32[2,128,128]{1,2,0:T(8,128)S(1)} custom-call(f32[2,128,128]{2,1,0:T(8,128)S(1)} %get-tuple-element.649), custom_call_target="InvertDiagBlocksLowerTriangular" | custom-call | tf_op jit(solution)/shard_map/jit(_solve_triangular)/triangular_solve | solution.py:43
  135.7 33.3 %all-reduce.36.cloned.1.call-done = f32[2,256,256]{2,1,0:T(8,128)} async-done(((f32[2,256,256]{2,1,0:T(8,128)}), f32[2,256,256]{2,1,0:T(8,128)}) %all-reduce.36.cloned.1.call-update) | async-done | bytes 524304 | tf_op jit(solution)/shard_map/psum | solution.py:9
  171.9 55.2 %all-reduce.80.cloned.1.call-done = (f32[256,256]{1,0:T(8,128)}, f32[256,256]{1,0:T(8,128)}) async-done(((f32[256,256]{1,0:T(8,128)}, f32[256,256]{1,0:T(8,128)}), (f32[256,256]{1,0:T(8,128)}, f32[256,256]{1,0:T(8,128)})) %all-reduce.80.cloned.1.call-update) | async-done | bytes 524304 | tf_op jit(solution)/shard_map/psum | solution.py:9
  230.1 54.3 %all-reduce.38.cloned.1.call-done = f32[256,256]{1,0:T(8,128)} async-done(((f32[256,256]{1,0:T(8,128)}), f32[256,256]{1,0:T(8,128)}) %all-reduce.38.cloned.1.call-update) | async-done | bytes 262160 | tf_op jit(solution)/shard_map/psum | solution.py:9
  285.9 11.7 cholesky.416
  297.7 9.8 custom-call.27
  308.2 11.7 cholesky.433
  322.7 4.3 while.41
  327.0 19.7 %custom-call.28 = f32[2,128,128]{1,2,0:T(8,128)S(1)} custom-call(f32[2,128,128]{2,1,0:T(8,128)S(1)} %get-tuple-element.650), custom_call_target="InvertDiagBlocksLowerTriangular" | custom-call | tf_op jit(solution)/shard_map/jit(_solve_triangular)/triangular_solve | solution.py:43
  350.5 36.5 %all-reduce.40.cloned.1.call-done = f32[2,256,256]{2,1,0:T(8,128)} async-done(((f32[2,256,256]{2,1,0:T(8,128)}), f32[2,256,256]{2,1,0:T(8,128)}) %all-reduce.40.cloned.1.call-update) | async-done | bytes 524304 | tf_op jit(solution)/shard_map/psum | solution.py:9
  390.0 55.0 %all-reduce.78.cloned.1.call-done = (f32[256,256]{1,0:T(8,128)}, f32[256,256]{1,0:T(8,128)}) async-done(((f32[256,256]{1,0:T(8,128)}, f32[256,256]{1,0:T(8,128)}), (f32[256,256]{1,0:T(8,128)}, f32[256,256]{1,0:T(8,128)})) %all-reduce.78.cloned.1.call-update) | async-done | bytes 524304 | tf_op jit(solution)/shard_map/psum | solution.py:9
  448.0 54.3 %all-reduce.42.cloned.1.call-done = f32[256,256]{1,0:T(8,128)} async-done(((f32[256,256]{1,0:T(8,128)}), f32[256,256]{1,0:T(8,128)}) %all-reduce.42.cloned.1.call-update) | async-done | bytes 262160 | tf_op jit(solution)/shard_map/psum | solution.py:9
  503.8 11.7 cholesky.450
  515.6 9.8 custom-call.29
  526.1 11.7 cholesky.467
  540.6 4.5 while.42
  545.1 19.7 %custom-call.30 = f32[2,128,128]{1,2,0:T(8,128)S(1)} custom-call(f32[2,128,128]{2,1,0:T(8,128)S(1)} %get-tuple-element.651), custom_call_target="InvertDiagBlocksLowerTriangular" | custom-call | tf_op jit(solution)/shard_map/jit(_solve_triangular)/triangular_solve | solution.py:43
  568.6 36.5 %all-reduce.44.cloned.1.call-done = f32[2,256,256]{2,1,0:T(8,128)} async-done(((f32[2,256,256]{2,1,0:T(8,128)}), f32[2,256,256]{2,1,0:T(8,128)}) %all-reduce.44.cloned.1.call-update) | async-done | bytes 524304 | tf_op jit(solution)/shard_map/psum | solution.py:9
  608.1 55.2 %all-reduce.76.cloned.1.call-done = (f32[256,256]{1,0:T(8,128)}, f32[256,256]{1,0:T(8,128)}) async-done(((f32[256,256]{1,0:T(8,128)}, f32[256,256]{1,0:T(8,128)}), (f32[256,256]{1,0:T(8,128)}, f32[256,256]{1,0:T(8,128)})) %all-reduce.76.cloned.1.call-update) | async-done | bytes 524304 | tf_op jit(solution)/shard_map/psum | solution.py:9
  666.2 54.4 %all-reduce.46.cloned.1.call-done = f32[256,256]{1,0:T(8,128)} async-done(((f32[256,256]{1,0:T(8,128)}), f32[256,256]{1,0:T(8,128)}) %all-reduce.46.cloned.1.call-update) | async-done | bytes 262160 | tf_op jit(solution)/shard_map/psum | solution.py:9
  722.1 11.7 cholesky.484
  733.9 9.8 custom-call.31
  744.3 11.7 cholesky.501
  758.8 4.3 while.43
  763.1 19.7 %custom-call.32 = f32[2,128,128]{1,2,0:T(8,128)S(1)} custom-call(f32[2,128,128]{2,1,0:T(8,128)S(1)} %get-tuple-element.652), custom_call_target="InvertDiagBlocksLowerTriangular" | custom-call | tf_op jit(solution)/shard_map/jit(_solve_triangular)/triangular_solve | solution.py:43
  786.7 36.4 %all-reduce.48.cloned.1.call-done = f32[2,256,256]{2,1,0:T(8,128)} async-done(((f32[2,256,256]{2,1,0:T(8,128)}), f32[2,256,256]{2,1,0:T(8,128)}) %all-reduce.48.cloned.1.call-update) | async-done | bytes 524304 | tf_op jit(solution)/shard_map/psum | solution.py:9
  826.1 55.0 %all-reduce.74.cloned.1.call-done = (f32[256,256]{1,0:T(8,128)}, f32[256,256]{1,0:T(8,128)}) async-done(((f32[256,256]{1,0:T(8,128)}, f32[256,256]{1,0:T(8,128)}), (f32[256,256]{1,0:T(8,128)}, f32[256,256]{1,0:T(8,128)})) %all-reduce.74.cloned.1.call-update) | async-done | bytes 524304 | tf_op jit(solution)/shard_map/psum | solution.py:9
  884.0 53.0 %all-reduce.50.cloned.1.call-done = f32[256,256]{1,0:T(8,128)} async-done(((f32[256,256]{1,0:T(8,128)}), f32[256,256]{1,0:T(8,128)}) %all-reduce.50.cloned.1.call-update) | async-done | bytes 262160 | tf_op jit(solution)/shard_map/psum | solution.py:9
  938.5 11.7 cholesky.518
  950.3 9.8 custom-call.33
  960.7 11.7 cholesky.535
  975.2 4.5 while.44
  979.8 19.7 %custom-call.34 = f32[2,128,128]{1,2,0:T(8,128)S(1)} custom-call(f32[2,128,128]{2,1,0:T(8,128)S(1)} %get-tuple-element.653), custom_call_target="InvertDiagBlocksLowerTriangular" | custom-call | tf_op jit(solution)/shard_map/jit(_solve_triangular)/triangular_solve | solution.py:43
  1003.3 36.4 %all-reduce.52.cloned.1.call-done = f32[2,256,256]{2,1,0:T(8,128)} async-done(((f32[2,256,256]{2,1,0:T(8,128)}), f32[2,256,256]{2,1,0:T(8,128)}) %all-reduce.52.cloned.1.call-update) | async-done | bytes 524304 | tf_op jit(solution)/shard_map/psum | solution.py:9
  1042.7 55.0 %all-reduce.72.cloned.1.call-done = (f32[256,256]{1,0:T(8,128)}, f32[256,256]{1,0:T(8,128)}) async-done(((f32[256,256]{1,0:T(8,128)}, f32[256,256]{1,0:T(8,128)}), (f32[256,256]{1,0:T(8,128)}, f32[256,256]{1,0:T(8,128)})) %all-reduce.72.cloned.1.call-update) | async-done | bytes 524304 | tf_op jit(solution)/shard_map/psum | solution.py:9
  1099.8 53.6 %all-reduce.54.cloned.1.call-done = f32[256,256]{1,0:T(8,128)} async-done(((f32[256,256]{1,0:T(8,128)}), f32[256,256]{1,0:T(8,128)}) %all-reduce.54.cloned.1.call-update) | async-done | bytes 262160 | tf_op jit(solution)/shard_map/psum | solution.py:9
  1154.9 11.7 cholesky.552
  1166.7 9.8 custom-call.35
  1177.2 11.7 cholesky.569
  1191.7 4.3 while.45
  1196.0 19.7 %custom-call.36 = f32[2,128,128]{1,2,0:T(8,128)S(1)} custom-call(f32[2,128,128]{2,1,0:T(8,128)S(1)} %get-tuple-element.654), custom_call_target="InvertDiagBlocksLowerTriangular" | custom-call | tf_op jit(solution)/shard_map/jit(_solve_triangular)/triangular_solve | solution.py:43
  1219.5 36.4 %all-reduce.56.cloned.1.call-done = f32[2,256,256]{2,1,0:T(8,128)} async-done(((f32[2,256,256]{2,1,0:T(8,128)}), f32[2,256,256]{2,1,0:T(8,128)}) %all-reduce.56.cloned.1.call-update) | async-done | bytes 524304 | tf_op jit(solution)/shard_map/psum | solution.py:9
  1258.9 55.0 %all-reduce.70.cloned.1.call-done = (f32[256,256]{1,0:T(8,128)}, f32[256,256]{1,0:T(8,128)}) async-done(((f32[256,256]{1,0:T(8,128)}, f32[256,256]{1,0:T(8,128)}), (f32[256,256]{1,0:T(8,128)}, f32[256,256]{1,0:T(8,128)})) %all-reduce.70.cloned.1.call-update) | async-done | bytes 524304 | tf_op jit(solution)/shard_map/psum | solution.py:9
  1316.2 53.6 %all-reduce.58.cloned.1.call-done = f32[256,256]{0,1:T(8,128)} async-done(((f32[256,256]{0,1:T(8,128)}), f32[256,256]{0,1:T(8,128)}) %all-reduce.58.cloned.1.call-update) | async-done | bytes 262160 | tf_op jit(solution)/shard_map/psum | solution.py:9
  1371.3 11.7 cholesky.586
  1383.1 9.8 custom-call.37
  1393.6 11.7 cholesky.603
  1408.1 4.5 while.46
  1412.6 19.7 %custom-call.38 = f32[2,128,128]{1,2,0:T(8,128)S(1)} custom-call(f32[2,128,128]{2,1,0:T(8,128)S(1)} %get-tuple-element.655), custom_call_target="InvertDiagBlocksLowerTriangular" | custom-call | tf_op jit(solution)/shard_map/jit(_solve_triangular)/triangular_solve | solution.py:43
  1436.1 36.4 %all-reduce.60.cloned.1.call-done = f32[2,256,256]{2,1,0:T(8,128)} async-done(((f32[2,256,256]{2,1,0:T(8,128)}), f32[2,256,256]{2,1,0:T(8,128)}) %all-reduce.60.cloned.1.call-update) | async-done | bytes 524304 | tf_op jit(solution)/shard_map/psum | solution.py:9
  1475.5 55.1 %all-reduce.68.cloned.1.call-done = (f32[256,256]{1,0:T(8,128)}, f32[256,256]{1,0:T(8,128)}) async-done(((f32[256,256]{1,0:T(8,128)}, f32[256,256]{1,0:T(8,128)}), (f32[256,256]{1,0:T(8,128)}, f32[256,256]{1,0:T(8,128)})) %all-reduce.68.cloned.1.call-update) | async-done | bytes 524304 | tf_op jit(solution)/shard_map/psum | solution.py:9
  1533.0 53.5 %all-reduce.62.cloned.1.call-done = f32[256,256]{1,0:T(8,128)} async-done(((f32[256,256]{1,0:T(8,128)}), f32[256,256]{1,0:T(8,128)}) %all-reduce.62.cloned.1.call-update) | async-done | bytes 262160 | tf_op jit(solution)/shard_map/psum | solution.py:9
  1588.7 11.7 cholesky.620
  1600.5 9.8 custom-call.39
  1610.8 11.7 cholesky.637
  1625.3 4.3 while.47
  1629.6 19.7 %custom-call.40 = f32[2,128,128]{1,2,0:T(8,128)S(1)} custom-call(f32[2,128,128]{2,1,0:T(8,128)S(1)} %get-tuple-element.656), custom_call_target="InvertDiagBlocksLowerTriangular" | custom-call | tf_op jit(solution)/shard_map/jit(_solve_triangular)/triangular_solve | solution.py:43
  1653.1 36.4 %all-reduce.64.cloned.1.call-done = f32[2,256,256]{2,1,0:T(8,128)} async-done(((f32[2,256,256]{2,1,0:T(8,128)}), f32[2,256,256]{2,1,0:T(8,128)}) %all-reduce.64.cloned.1.call-update) | async-done | bytes 524304 | tf_op jit(solution)/shard_map/psum | solution.py:9
  1692.5 55.0 %all-reduce.66.cloned.1.call-done = (f32[256,256]{1,0:T(8,128)}, f32[256,256]{1,0:T(8,128)}) async-done(((f32[256,256]{1,0:T(8,128)}, f32[256,256]{1,0:T(8,128)}), (f32[256,256]{1,0:T(8,128)}, f32[256,256]{1,0:T(8,128)})) %all-reduce.66.cloned.1.call-update) | async-done | bytes 524304 | tf_op jit(solution)/shard_map/psum | solution.py:9
  (461 shorter events, 133.3 us)
Async XLA Ops:
  6.5 1.6 copy-start.8
  6.5 60.1 %all-reduce.34.cloned.1.call-start = ((), (), s32[]{:S(2)}) async-start(), calls=%async_computation | async-start | bytes 524288 | tf_op jit(solution)/shard_map/psum | solution.py:9
  9.2 159.8 %all-reduce.36.cloned.1.call-start = ((), (), s32[]{:S(2)}) async-start(), calls=%async_computation.1 | async-start | bytes 1048576 | tf_op jit(solution)/shard_map/psum | solution.py:9
  66.7 1.2 copy-start.10
  131.1 96.0 %all-reduce.80.cloned.1.call-start = ((), (), s32[]{:S(2)}) async-start(), calls=%async_computation.23 | async-start | bytes 1048576 | tf_op jit(solution)/shard_map/psum | solution.py:9
  171.7 112.7 %all-reduce.38.cloned.1.call-start = ((), (), s32[]{:S(2)}) async-start(), calls=%async_computation.2 | async-start | bytes 524288 | tf_op jit(solution)/shard_map/psum | solution.py:9
  171.7 55.4 %copy-start = (f32[2,256,256]{2,1,0:T(8,128)S(1)}, f32[2,256,256]{2,1,0:T(8,128)}, u32[]{:S(2)}) copy-start(f32[2,256,256]{2,1,0:T(8,128)} %all-reduce.36.cloned.1.call-done) | copy-start | bytes 1572868
  227.1 1.0 copy-start.21
  229.8 157.2 %all-reduce.40.cloned.1.call-start = ((), (), s32[]{:S(2)}) async-start(), calls=%async_computation.3 | async-start | bytes 1048576 | tf_op jit(solution)/shard_map/psum | solution.py:9
  284.4 1.2 copy-start.12
  349.1 95.8 %all-reduce.78.cloned.1.call-start = ((), (), s32[]{:S(2)}) async-start(), calls=%async_computation.22 | async-start | bytes 1048576 | tf_op jit(solution)/shard_map/psum | solution.py:9
  389.7 112.6 %all-reduce.42.cloned.1.call-start = ((), (), s32[]{:S(2)}) async-start(), calls=%async_computation.4 | async-start | bytes 524288 | tf_op jit(solution)/shard_map/psum | solution.py:9
  389.8 55.2 %copy-start.7 = (f32[2,256,256]{2,1,0:T(8,128)S(1)}, f32[2,256,256]{2,1,0:T(8,128)}, u32[]{:S(2)}) copy-start(f32[2,256,256]{2,1,0:T(8,128)} %all-reduce.40.cloned.1.call-done) | copy-start | bytes 1572868
  445.0 1.0 copy-start.22
  447.6 157.4 %all-reduce.44.cloned.1.call-start = ((), (), s32[]{:S(2)}) async-start(), calls=%async_computation.5 | async-start | bytes 1048576 | tf_op jit(solution)/shard_map/psum | solution.py:9
  502.3 1.2 copy-start.13
  567.3 96.0 %all-reduce.76.cloned.1.call-start = ((), (), s32[]{:S(2)}) async-start(), calls=%async_computation.21 | async-start | bytes 1048576 | tf_op jit(solution)/shard_map/psum | solution.py:9
  607.8 112.7 %all-reduce.46.cloned.1.call-start = ((), (), s32[]{:S(2)}) async-start(), calls=%async_computation.6 | async-start | bytes 524288 | tf_op jit(solution)/shard_map/psum | solution.py:9
  607.9 55.4 %copy-start.5 = (f32[2,256,256]{2,1,0:T(8,128)S(1)}, f32[2,256,256]{2,1,0:T(8,128)}, u32[]{:S(2)}) copy-start(f32[2,256,256]{2,1,0:T(8,128)} %all-reduce.44.cloned.1.call-done) | copy-start | bytes 1572868
  663.3 1.0 copy-start.23
  665.9 157.2 %all-reduce.48.cloned.1.call-start = ((), (), s32[]{:S(2)}) async-start(), calls=%async_computation.7 | async-start | bytes 1048576 | tf_op jit(solution)/shard_map/psum | solution.py:9
  720.6 1.2 copy-start.11
  785.3 95.8 %all-reduce.74.cloned.1.call-start = ((), (), s32[]{:S(2)}) async-start(), calls=%async_computation.20 | async-start | bytes 1048576 | tf_op jit(solution)/shard_map/psum | solution.py:9
  825.8 111.1 %all-reduce.50.cloned.1.call-start = ((), (), s32[]{:S(2)}) async-start(), calls=%async_computation.8 | async-start | bytes 524288 | tf_op jit(solution)/shard_map/psum | solution.py:9
  825.9 55.2 %copy-start.6 = (f32[2,256,256]{2,1,0:T(8,128)S(1)}, f32[2,256,256]{2,1,0:T(8,128)}, u32[]{:S(2)}) copy-start(f32[2,256,256]{2,1,0:T(8,128)} %all-reduce.48.cloned.1.call-done) | copy-start | bytes 1572868
  881.1 1.0 copy-start.24
  883.7 156.0 %all-reduce.52.cloned.1.call-start = ((), (), s32[]{:S(2)}) async-start(), calls=%async_computation.9 | async-start | bytes 1048576 | tf_op jit(solution)/shard_map/psum | solution.py:9
  937.0 1.2 copy-start.14
  1001.9 95.8 %all-reduce.72.cloned.1.call-start = ((), (), s32[]{:S(2)}) async-start(), calls=%async_computation.19 | async-start | bytes 1048576 | tf_op jit(solution)/shard_map/psum | solution.py:9
  1042.4 111.0 %all-reduce.54.cloned.1.call-start = ((), (), s32[]{:S(2)}) async-start(), calls=%async_computation.10 | async-start | bytes 524288 | tf_op jit(solution)/shard_map/psum | solution.py:9
  1042.6 55.0 %copy-start.2 = (f32[2,256,256]{2,1,0:T(8,128)S(1)}, f32[2,256,256]{2,1,0:T(8,128)}, u32[]{:S(2)}) copy-start(f32[2,256,256]{2,1,0:T(8,128)} %all-reduce.52.cloned.1.call-done) | copy-start | bytes 1572868
  1097.7 1.0 copy-start.17
  1099.5 156.4 %all-reduce.56.cloned.1.call-start = ((), (), s32[]{:S(2)}) async-start(), calls=%async_computation.11 | async-start | bytes 1048576 | tf_op jit(solution)/shard_map/psum | solution.py:9
  1153.4 1.2 copy-start.15
  1218.1 95.8 %all-reduce.70.cloned.1.call-start = ((), (), s32[]{:S(2)}) async-start(), calls=%async_computation.18 | async-start | bytes 1048576 | tf_op jit(solution)/shard_map/psum | solution.py:9
  1258.7 111.1 %all-reduce.58.cloned.1.call-start = ((), (), s32[]{:S(2)}) async-start(), calls=%async_computation.12 | async-start | bytes 524288 | tf_op jit(solution)/shard_map/psum | solution.py:9
  1258.9 55.0 %copy-start.3 = (f32[2,256,256]{2,1,0:T(8,128)S(1)}, f32[2,256,256]{2,1,0:T(8,128)}, u32[]{:S(2)}) copy-start(f32[2,256,256]{2,1,0:T(8,128)} %all-reduce.56.cloned.1.call-done) | copy-start | bytes 1572868
  1314.0 1.0 copy-start.18
  1315.9 156.6 %all-reduce.60.cloned.1.call-start = ((), (), s32[]{:S(2)}) async-start(), calls=%async_computation.13 | async-start | bytes 1048576 | tf_op jit(solution)/shard_map/psum | solution.py:9
  1369.8 1.2 copy-start.16
  1434.7 96.0 %all-reduce.68.cloned.1.call-start = ((), (), s32[]{:S(2)}) async-start(), calls=%async_computation.17 | async-start | bytes 1048576 | tf_op jit(solution)/shard_map/psum | solution.py:9
  1475.3 111.3 %all-reduce.62.cloned.1.call-start = ((), (), s32[]{:S(2)}) async-start(), calls=%async_computation.14 | async-start | bytes 524288 | tf_op jit(solution)/shard_map/psum | solution.py:9
  1475.5 55.2 %copy-start.4 = (f32[2,256,256]{2,1,0:T(8,128)S(1)}, f32[2,256,256]{2,1,0:T(8,128)}, u32[]{:S(2)}) copy-start(f32[2,256,256]{2,1,0:T(8,128)} %all-reduce.60.cloned.1.call-done) | copy-start | bytes 1572868
  1530.7 1.0 copy-start.19
  1532.5 157.0 %all-reduce.64.cloned.1.call-start = ((), (), s32[]{:S(2)}) async-start(), calls=%async_computation.15 | async-start | bytes 1048576 | tf_op jit(solution)/shard_map/psum | solution.py:9
  1587.5 1.0 copy-start.9
  1651.7 95.8 %all-reduce.66.cloned.1.call-start = ((), (), s32[]{:S(2)}) async-start(), calls=%async_computation.16 | async-start | bytes 1048576 | tf_op jit(solution)/shard_map/psum | solution.py:9
  1692.4 55.1 %copy-start.1 = (f32[2,256,256]{2,1,0:T(8,128)S(1)}, f32[2,256,256]{2,1,0:T(8,128)}, u32[]{:S(2)}) copy-start(f32[2,256,256]{2,1,0:T(8,128)} %all-reduce.64.cloned.1.call-done) | copy-start | bytes 1572868
  1747.5 1.0 copy-start.20
Sparse Core Ops, SparseCore 0:
  10.4 56.2 all-reduce.33
  131.2 37.6 all-reduce.35
  172.4 54.6 all-reduce.79
  230.0 54.3 all-reduce.37
  349.3 37.6 all-reduce.39
  390.3 54.6 all-reduce.77
  448.0 54.2 all-reduce.41
  567.4 37.6 all-reduce.43
  608.5 54.6 all-reduce.75
  666.1 54.3 all-reduce.45
  785.4 37.6 all-reduce.47
  826.4 54.6 all-reduce.73
  884.1 52.7 all-reduce.49
  1002.0 37.6 all-reduce.51
  1043.0 54.6 all-reduce.71
  1100.6 52.7 all-reduce.53
  1218.2 37.6 all-reduce.55
  1259.2 54.6 all-reduce.69
  1317.0 52.7 all-reduce.57
  1434.8 37.6 all-reduce.59
  1476.0 54.6 all-reduce.67
  1533.7 52.7 all-reduce.61
  1651.8 37.6 all-reduce.63
  1692.8 54.6 all-reduce.65
where the time goes:
time: 1770 us; the launch traced here: 1760 us
  waiting for transfers between devices  1160 us (66%)
  other arithmetic  477 us (27%)
  local copies, waits for them, and re-layouts  58.3 us (3%)
  between operations  38.5 us (2%)
    psum x24, waiting for transfers between devices, from_root(): return lax.psum(kept, axis)  1160 us
    another operation x55, other arithmetic, shards(): lower_factor = jnp.linalg.cholesky(symmetric)  277 us
    another operation x17, other arithmetic, shards(): jax.scipy.linalg.solve_triangular(lower_factor, flattened.T, lower=True)  158 us
  transfers between devices with their start and end apart: 24, of which 24 were waited for; matrix products, arithmetic and copies ran while one was open for 0% of the time, Pallas kernels for 0%

commit v1 on v0

--- a/solution.py
+++ b/solution.py
@@ -6,7 +6,7 @@
 
 def from_root(value, axis, source):
     kept = jnp.where(lax.axis_index(axis) == source, value, 0).astype(value.dtype)
-    return lax.psum(kept, axis)
+    return jax.lax.all_gather(kept, axis_name=axis).sum(axis=0)
 
 
 def pick_tile(tiles, tile_rows, wanted):

time: 1770 us -> 1710 us (0.966)
  waiting for transfers between devices: 1160 us -> 1020 us
  local copies, waits for them, and re-layouts: 58.3 us -> 108 us
  other arithmetic: 477 us -> 522 us
    psum x24 -> x0, waiting for transfers between devices: 1160 us -> none  [from_root(): return lax.psum(kept, axis)]
    all_gather x0 -> x32, waiting for transfers between devices: none -> 1010 us  [from_root(): return jax.lax.all_gather(kept, axis_name=axis).sum(axis=0)]
    reduce_sum x0 -> x20, other arithmetic: none -> 25.6 us  [from_root(): return jax.lax.all_gather(kept, axis_name=axis).sum(axis=0)]
  transfers between devices with their start and end apart: 24 -> 32, of which waited for: 24 -> 32; matrix products, arithmetic and copies ran while one was open for 0% -> 2% of each run, Pallas kernels for 0% -> 0%
where the time goes in v1:
time: 1710 us; the launch traced here: 1700 us
  waiting for transfers between devices  1020 us (60%)
  other arithmetic  522 us (31%)
  local copies, waits for them, and re-layouts  108 us (6%)
  between operations  37.7 us (2%)
    all_gather x32, waiting for transfers between devices, from_root(): return jax.lax.all_gather(kept, axis_name=axis).sum(axis=0)  1010 us
    another operation x55, other arithmetic, shards(): lower_factor = jnp.linalg.cholesky(symmetric)  279 us
    another operation x17, other arithmetic, shards(): jax.scipy.linalg.solve_triangular(lower_factor, flattened.T, lower=True)  158 us
  transfers between devices with their start and end apart: 32, of which 32 were waited for; matrix products, arithmetic and copies ran while one was open for 2% of the time, Pallas kernels for 0%

profile of v1, /device:TPU:0, one launch (start us, length us, event | category | flops | bytes accessed | tf_op | source)
XLA Modules:
  0.0 1702.9 jit_solution(11273299532167243053)
XLA Ops:
  12.7 30.7 %all-gather.73.cloned.1.call-done = f32[2048,256]{0,1:T(8,128)} async-done(((f32[256,256]{0,1:T(8,128)}), f32[2048,256]{0,1:T(8,128)}) %all-gather.73.cloned.1.call-update) | async-done | bytes 2097168 | tf_op jit(solution)/shard_map/all_gather | solution.py:9
  46.9 11.7 cholesky.382
  58.7 9.8 custom-call.25
  68.9 11.7 cholesky.399
  87.3 19.7 %custom-call.26 = f32[2,128,128]{1,2,0:T(8,128)S(1)} custom-call(f32[2,128,128]{2,1,0:T(8,128)S(1)} %get-tuple-element.681), custom_call_target="InvertDiagBlocksLowerTriangular" | custom-call | tf_op jit(solution)/shard_map/jit(_solve_triangular)/triangular_solve | solution.py:43
  111.9 43.6 %all-gather.57.cloned.1.call-done = f32[4,2,256,256]{3,2,1,0:T(8,128)} async-done(((f32[1,2,256,256]{3,2,1,0:T(8,128)}), f32[4,2,256,256]{3,2,1,0:T(8,128)}) %all-gather.57.cloned.1.call-update) | async-done | bytes 2097168 | tf_op jit(solution)/shard_map/all_gather | solution.py:9
  166.2 20.6 %all-gather.75.cloned.1.call-done = f32[2048,256]{0,1:T(8,128)} async-done(((f32[256,256]{0,1:T(8,128)}), f32[2048,256]{0,1:T(8,128)}) %all-gather.75.cloned.1.call-update) | async-done | bytes 2097168 | tf_op jit(solution)/shard_map/all_gather | solution.py:9
  187.9 28.8 %all-gather.77.cloned.1.call-done = f32[2048,256]{0,1:T(8,128)} async-done(((f32[256,256]{0,1:T(8,128)}), f32[2048,256]{0,1:T(8,128)}) %all-gather.77.cloned.1.call-update) | async-done | bytes 2097168 | tf_op jit(solution)/shard_map/all_gather | solution.py:9
  226.7 27.9 %all-gather.79.cloned.1.call-done = f32[2048,256]{0,1:T(8,128)} async-done(((f32[256,256]{0,1:T(8,128)}), f32[2048,256]{0,1:T(8,128)}) %all-gather.79.cloned.1.call-update) | async-done | bytes 2097168 | tf_op jit(solution)/shard_map/all_gather | solution.py:9
  258.0 11.7 cholesky.416
  269.8 9.8 custom-call.27
  280.1 11.7 cholesky.433
  299.1 19.7 %custom-call.28 = f32[2,128,128]{1,2,0:T(8,128)S(1)} custom-call(f32[2,128,128]{2,1,0:T(8,128)S(1)} %get-tuple-element.682), custom_call_target="InvertDiagBlocksLowerTriangular" | custom-call | tf_op jit(solution)/shard_map/jit(_solve_triangular)/triangular_solve | solution.py:43
  321.3 46.0 %all-gather.59.cloned.1.call-done = f32[4,2,256,256]{3,2,1,0:T(8,128)} async-done(((f32[1,2,256,256]{3,2,1,0:T(8,128)}), f32[4,2,256,256]{3,2,1,0:T(8,128)}) %all-gather.59.cloned.1.call-update) | async-done | bytes 2097168 | tf_op jit(solution)/shard_map/all_gather | solution.py:9
  377.3 21.3 %all-gather.81.cloned.1.call-done = f32[2048,256]{0,1:T(8,128)} async-done(((f32[256,256]{0,1:T(8,128)}), f32[2048,256]{0,1:T(8,128)}) %all-gather.81.cloned.1.call-update) | async-done | bytes 2097168 | tf_op jit(solution)/shard_map/all_gather | solution.py:9
  399.7 29.0 %all-gather.83.cloned.1.call-done = f32[2048,256]{0,1:T(8,128)} async-done(((f32[256,256]{0,1:T(8,128)}), f32[2048,256]{0,1:T(8,128)}) %all-gather.83.cloned.1.call-update) | async-done | bytes 2097168 | tf_op jit(solution)/shard_map/all_gather | solution.py:9
  438.6 27.9 %all-gather.85.cloned.1.call-done = f32[2048,256]{0,1:T(8,128)} async-done(((f32[256,256]{0,1:T(8,128)}), f32[2048,256]{0,1:T(8,128)}) %all-gather.85.cloned.1.call-update) | async-done | bytes 2097168 | tf_op jit(solution)/shard_map/all_gather | solution.py:9
  469.9 11.7 cholesky.450
  481.7 9.8 custom-call.29
  492.0 11.7 cholesky.467
  511.0 19.7 %custom-call.30 = f32[2,128,128]{1,2,0:T(8,128)S(1)} custom-call(f32[2,128,128]{2,1,0:T(8,128)S(1)} %get-tuple-element.683), custom_call_target="InvertDiagBlocksLowerTriangular" | custom-call | tf_op jit(solution)/shard_map/jit(_solve_triangular)/triangular_solve | solution.py:43
  533.2 46.0 %all-gather.61.cloned.1.call-done = f32[4,2,256,256]{3,2,1,0:T(8,128)} async-done(((f32[1,2,256,256]{3,2,1,0:T(8,128)}), f32[4,2,256,256]{3,2,1,0:T(8,128)}) %all-gather.61.cloned.1.call-update) | async-done | bytes 2097168 | tf_op jit(solution)/shard_map/all_gather | solution.py:9
  589.2 21.3 %all-gather.87.cloned.1.call-done = f32[2048,256]{0,1:T(8,128)} async-done(((f32[256,256]{0,1:T(8,128)}), f32[2048,256]{0,1:T(8,128)}) %all-gather.87.cloned.1.call-update) | async-done | bytes 2097168 | tf_op jit(solution)/shard_map/all_gather | solution.py:9
  611.6 28.8 %all-gather.89.cloned.1.call-done = f32[2048,256]{0,1:T(8,128)} async-done(((f32[256,256]{0,1:T(8,128)}), f32[2048,256]{0,1:T(8,128)}) %all-gather.89.cloned.1.call-update) | async-done | bytes 2097168 | tf_op jit(solution)/shard_map/all_gather | solution.py:9
  650.3 27.9 %all-gather.91.cloned.1.call-done = f32[2048,256]{0,1:T(8,128)} async-done(((f32[256,256]{0,1:T(8,128)}), f32[2048,256]{0,1:T(8,128)}) %all-gather.91.cloned.1.call-update) | async-done | bytes 2097168 | tf_op jit(solution)/shard_map/all_gather | solution.py:9
  681.7 11.7 cholesky.484
  693.4 9.8 custom-call.31
  703.7 11.7 cholesky.501
  722.7 19.7 %custom-call.32 = f32[2,128,128]{1,2,0:T(8,128)S(1)} custom-call(f32[2,128,128]{2,1,0:T(8,128)S(1)} %get-tuple-element.684), custom_call_target="InvertDiagBlocksLowerTriangular" | custom-call | tf_op jit(solution)/shard_map/jit(_solve_triangular)/triangular_solve | solution.py:43
  744.9 46.0 %all-gather.63.cloned.1.call-done = f32[4,2,256,256]{3,2,1,0:T(8,128)} async-done(((f32[1,2,256,256]{3,2,1,0:T(8,128)}), f32[4,2,256,256]{3,2,1,0:T(8,128)}) %all-gather.63.cloned.1.call-update) | async-done | bytes 2097168 | tf_op jit(solution)/shard_map/all_gather | solution.py:9
  800.9 21.3 %all-gather.93.cloned.1.call-done = f32[2048,256]{0,1:T(8,128)} async-done(((f32[256,256]{0,1:T(8,128)}), f32[2048,256]{0,1:T(8,128)}) %all-gather.93.cloned.1.call-update) | async-done | bytes 2097168 | tf_op jit(solution)/shard_map/all_gather | solution.py:9
  823.3 28.8 %all-gather.95.cloned.1.call-done = f32[2048,256]{0,1:T(8,128)} async-done(((f32[256,256]{0,1:T(8,128)}), f32[2048,256]{0,1:T(8,128)}) %all-gather.95.cloned.1.call-update) | async-done | bytes 2097168 | tf_op jit(solution)/shard_map/all_gather | solution.py:9
  860.1 27.7 %all-gather.97.cloned.1.call-done = f32[2048,256]{0,1:T(8,128)} async-done(((f32[256,256]{0,1:T(8,128)}), f32[2048,256]{0,1:T(8,128)}) %all-gather.97.cloned.1.call-update) | async-done | bytes 2097168 | tf_op jit(solution)/shard_map/all_gather | solution.py:9
  891.2 11.7 cholesky.518
  903.0 9.8 custom-call.33
  913.3 12.1 cholesky.535
  932.3 19.7 %custom-call.34 = f32[2,128,128]{1,2,0:T(8,128)S(1)} custom-call(f32[2,128,128]{2,1,0:T(8,128)S(1)} %get-tuple-element.685), custom_call_target="InvertDiagBlocksLowerTriangular" | custom-call | tf_op jit(solution)/shard_map/jit(_solve_triangular)/triangular_solve | solution.py:43
  954.5 46.0 %all-gather.65.cloned.1.call-done = f32[4,2,256,256]{3,2,1,0:T(8,128)} async-done(((f32[1,2,256,256]{3,2,1,0:T(8,128)}), f32[4,2,256,256]{3,2,1,0:T(8,128)}) %all-gather.65.cloned.1.call-update) | async-done | bytes 2097168 | tf_op jit(solution)/shard_map/all_gather | solution.py:9
  1008.8 22.9 %all-gather.99.cloned.1.call-done = f32[2048,256]{0,1:T(8,128)} async-done(((f32[256,256]{0,1:T(8,128)}), f32[2048,256]{0,1:T(8,128)}) %all-gather.99.cloned.1.call-update) | async-done | bytes 2097168 | tf_op jit(solution)/shard_map/all_gather | solution.py:9
  1032.9 28.9 %all-gather.101.cloned.1.call-done = f32[2048,256]{0,1:T(8,128)} async-done(((f32[256,256]{0,1:T(8,128)}), f32[2048,256]{0,1:T(8,128)}) %all-gather.101.cloned.1.call-update) | async-done | bytes 2097168 | tf_op jit(solution)/shard_map/all_gather | solution.py:9
  1064.1 33.2 %all-gather.103.cloned.1.call-done = f32[2048,256]{0,1:T(8,128)} async-done(((f32[256,256]{0,1:T(8,128)}), f32[2048,256]{0,1:T(8,128)}) %all-gather.103.cloned.1.call-update) | async-done | bytes 2097168 | tf_op jit(solution)/shard_map/all_gather | solution.py:9
  1100.8 11.7 cholesky.552
  1112.5 9.8 custom-call.35
  1122.8 12.1 cholesky.569
  1141.8 19.7 %custom-call.36 = f32[2,128,128]{1,2,0:T(8,128)S(1)} custom-call(f32[2,128,128]{2,1,0:T(8,128)S(1)} %get-tuple-element.686), custom_call_target="InvertDiagBlocksLowerTriangular" | custom-call | tf_op jit(solution)/shard_map/jit(_solve_triangular)/triangular_solve | solution.py:43
  1164.0 46.0 %all-gather.67.cloned.1.call-done = f32[4,2,256,256]{3,2,1,0:T(8,128)} async-done(((f32[1,2,256,256]{3,2,1,0:T(8,128)}), f32[4,2,256,256]{3,2,1,0:T(8,128)}) %all-gather.67.cloned.1.call-update) | async-done | bytes 2097168 | tf_op jit(solution)/shard_map/all_gather | solution.py:9
  1218.4 22.9 %all-gather.105.cloned.1.call-done = f32[2048,256]{0,1:T(8,128)} async-done(((f32[256,256]{0,1:T(8,128)}), f32[2048,256]{0,1:T(8,128)}) %all-gather.105.cloned.1.call-update) | async-done | bytes 2097168 | tf_op jit(solution)/shard_map/all_gather | solution.py:9
  1242.4 28.9 %all-gather.107.cloned.1.call-done = f32[2048,256]{0,1:T(8,128)} async-done(((f32[256,256]{0,1:T(8,128)}), f32[2048,256]{0,1:T(8,128)}) %all-gather.107.cloned.1.call-update) | async-done | bytes 2097168 | tf_op jit(solution)/shard_map/all_gather | solution.py:9
  1273.7 33.2 %all-gather.109.cloned.1.call-done = f32[2048,256]{0,1:T(8,128)} async-done(((f32[256,256]{0,1:T(8,128)}), f32[2048,256]{0,1:T(8,128)}) %all-gather.109.cloned.1.call-update) | async-done | bytes 2097168 | tf_op jit(solution)/shard_map/all_gather | solution.py:9
  1310.3 11.7 cholesky.586
  1322.1 9.8 custom-call.37
  1332.4 12.1 cholesky.603
  1351.4 19.7 %custom-call.38 = f32[2,128,128]{1,2,0:T(8,128)S(1)} custom-call(f32[2,128,128]{2,1,0:T(8,128)S(1)} %get-tuple-element.687), custom_call_target="InvertDiagBlocksLowerTriangular" | custom-call | tf_op jit(solution)/shard_map/jit(_solve_triangular)/triangular_solve | solution.py:43
  1373.6 46.0 %all-gather.69.cloned.1.call-done = f32[4,2,256,256]{3,2,1,0:T(8,128)} async-done(((f32[1,2,256,256]{3,2,1,0:T(8,128)}), f32[4,2,256,256]{3,2,1,0:T(8,128)}) %all-gather.69.cloned.1.call-update) | async-done | bytes 2097168 | tf_op jit(solution)/shard_map/all_gather | solution.py:9
  1428.0 22.9 %all-gather.111.cloned.1.call-done = f32[2048,256]{0,1:T(8,128)} async-done(((f32[256,256]{0,1:T(8,128)}), f32[2048,256]{0,1:T(8,128)}) %all-gather.111.cloned.1.call-update) | async-done | bytes 2097168 | tf_op jit(solution)/shard_map/all_gather | solution.py:9
  1452.0 29.0 %all-gather.113.cloned.1.call-done = f32[2048,256]{0,1:T(8,128)} async-done(((f32[256,256]{0,1:T(8,128)}), f32[2048,256]{0,1:T(8,128)}) %all-gather.113.cloned.1.call-update) | async-done | bytes 2097168 | tf_op jit(solution)/shard_map/all_gather | solution.py:9
  1483.4 33.2 %all-gather.115.cloned.1.call-done = f32[2048,256]{0,1:T(8,128)} async-done(((f32[256,256]{0,1:T(8,128)}), f32[2048,256]{0,1:T(8,128)}) %all-gather.115.cloned.1.call-update) | async-done | bytes 2097168 | tf_op jit(solution)/shard_map/all_gather | solution.py:9
  1520.0 11.7 cholesky.620
  1531.8 9.8 custom-call.39
  1542.1 11.9 cholesky.637
  1560.9 19.7 %custom-call.40 = f32[2,128,128]{1,2,0:T(8,128)S(1)} custom-call(f32[2,128,128]{2,1,0:T(8,128)S(1)} %get-tuple-element.688), custom_call_target="InvertDiagBlocksLowerTriangular" | custom-call | tf_op jit(solution)/shard_map/jit(_solve_triangular)/triangular_solve | solution.py:43
  1583.1 46.0 %all-gather.71.cloned.1.call-done = f32[4,2,256,256]{3,2,1,0:T(8,128)} async-done(((f32[1,2,256,256]{3,2,1,0:T(8,128)}), f32[4,2,256,256]{3,2,1,0:T(8,128)}) %all-gather.71.cloned.1.call-update) | async-done | bytes 2097168 | tf_op jit(solution)/shard_map/all_gather | solution.py:9
  1637.4 23.0 %all-gather.117.cloned.1.call-done = f32[2048,256]{0,1:T(8,128)} async-done(((f32[256,256]{0,1:T(8,128)}), f32[2048,256]{0,1:T(8,128)}) %all-gather.117.cloned.1.call-update) | async-done | bytes 2097168 | tf_op jit(solution)/shard_map/all_gather | solution.py:9
  1661.5 29.0 %all-gather.119.cloned.1.call-done = f32[2048,256]{0,1:T(8,128)} async-done(((f32[256,256]{0,1:T(8,128)}), f32[2048,256]{0,1:T(8,128)}) %all-gather.119.cloned.1.call-update) | async-done | bytes 2097168 | tf_op jit(solution)/shard_map/all_gather | solution.py:9
  (532 shorter events, 288.2 us)
Async XLA Ops:
  6.5 3.3 copy-start
  6.5 36.9 %all-gather.73.cloned.1.call-start = ((), (), s32[]{:S(2)}) async-start(), calls=%async_computation.8 | async-start | bytes 2359296 | tf_op jit(solution)/shard_map/all_gather | solution.py:9
  12.4 143.2 %all-gather.57.cloned.1.call-start = ((), (), s32[]{:S(2)}) async-start(), calls=%async_computation | async-start | bytes 2621440 | tf_op jit(solution)/shard_map/all_gather | solution.py:9
  109.5 77.3 %all-gather.75.cloned.1.call-start = ((), (), s32[]{:S(2)}) async-start(), calls=%async_computation.9 | async-start | bytes 2359296 | tf_op jit(solution)/shard_map/all_gather | solution.py:9
  159.7 57.0 %all-gather.77.cloned.1.call-start = ((), (), s32[]{:S(2)}) async-start(), calls=%async_computation.10 | async-start | bytes 2359296 | tf_op jit(solution)/shard_map/all_gather | solution.py:9
  161.2 93.4 %all-gather.79.cloned.1.call-start = ((), (), s32[]{:S(2)}) async-start(), calls=%async_computation.11 | async-start | bytes 2359296 | tf_op jit(solution)/shard_map/all_gather | solution.py:9
  226.2 141.1 %all-gather.59.cloned.1.call-start = ((), (), s32[]{:S(2)}) async-start(), calls=%async_computation.1 | async-start | bytes 2621440 | tf_op jit(solution)/shard_map/all_gather | solution.py:9
  321.2 77.3 %all-gather.81.cloned.1.call-start = ((), (), s32[]{:S(2)}) async-start(), calls=%async_computation.12 | async-start | bytes 2359296 | tf_op jit(solution)/shard_map/all_gather | solution.py:9
  371.5 57.2 %all-gather.83.cloned.1.call-start = ((), (), s32[]{:S(2)}) async-start(), calls=%async_computation.13 | async-start | bytes 2359296 | tf_op jit(solution)/shard_map/all_gather | solution.py:9
  372.3 94.2 %all-gather.85.cloned.1.call-start = ((), (), s32[]{:S(2)}) async-start(), calls=%async_computation.14 | async-start | bytes 2359296 | tf_op jit(solution)/shard_map/all_gather | solution.py:9
  438.1 141.1 %all-gather.61.cloned.1.call-start = ((), (), s32[]{:S(2)}) async-start(), calls=%async_computation.2 | async-start | bytes 2621440 | tf_op jit(solution)/shard_map/all_gather | solution.py:9
  533.1 77.3 %all-gather.87.cloned.1.call-start = ((), (), s32[]{:S(2)}) async-start(), calls=%async_computation.15 | async-start | bytes 2359296 | tf_op jit(solution)/shard_map/all_gather | solution.py:9
  583.4 57.1 %all-gather.89.cloned.1.call-start = ((), (), s32[]{:S(2)}) async-start(), calls=%async_computation.16 | async-start | bytes 2359296 | tf_op jit(solution)/shard_map/all_gather | solution.py:9
  584.2 94.1 %all-gather.91.cloned.1.call-start = ((), (), s32[]{:S(2)}) async-start(), calls=%async_computation.17 | async-start | bytes 2359296 | tf_op jit(solution)/shard_map/all_gather | solution.py:9
  649.9 141.1 %all-gather.63.cloned.1.call-start = ((), (), s32[]{:S(2)}) async-start(), calls=%async_computation.3 | async-start | bytes 2621440 | tf_op jit(solution)/shard_map/all_gather | solution.py:9
  744.9 77.3 %all-gather.93.cloned.1.call-start = ((), (), s32[]{:S(2)}) async-start(), calls=%async_computation.18 | async-start | bytes 2359296 | tf_op jit(solution)/shard_map/all_gather | solution.py:9
  795.1 57.0 %all-gather.95.cloned.1.call-start = ((), (), s32[]{:S(2)}) async-start(), calls=%async_computation.19 | async-start | bytes 2359296 | tf_op jit(solution)/shard_map/all_gather | solution.py:9
  795.9 91.8 %all-gather.97.cloned.1.call-start = ((), (), s32[]{:S(2)}) async-start(), calls=%async_computation.20 | async-start | bytes 2359296 | tf_op jit(solution)/shard_map/all_gather | solution.py:9
  859.4 141.1 %all-gather.65.cloned.1.call-start = ((), (), s32[]{:S(2)}) async-start(), calls=%async_computation.4 | async-start | bytes 2621440 | tf_op jit(solution)/shard_map/all_gather | solution.py:9
  954.4 77.4 %all-gather.99.cloned.1.call-start = ((), (), s32[]{:S(2)}) async-start(), calls=%async_computation.21 | async-start | bytes 2359296 | tf_op jit(solution)/shard_map/all_gather | solution.py:9
  1004.7 57.0 %all-gather.101.cloned.1.call-start = ((), (), s32[]{:S(2)}) async-start(), calls=%async_computation.22 | async-start | bytes 2359296 | tf_op jit(solution)/shard_map/all_gather | solution.py:9
  1005.5 91.8 %all-gather.103.cloned.1.call-start = ((), (), s32[]{:S(2)}) async-start(), calls=%async_computation.23 | async-start | bytes 2359296 | tf_op jit(solution)/shard_map/all_gather | solution.py:9
  1063.5 146.5 %all-gather.67.cloned.1.call-start = ((), (), s32[]{:S(2)}) async-start(), calls=%async_computation.5 | async-start | bytes 2621440 | tf_op jit(solution)/shard_map/all_gather | solution.py:9
  1164.0 77.4 %all-gather.105.cloned.1.call-start = ((), (), s32[]{:S(2)}) async-start(), calls=%async_computation.24 | async-start | bytes 2359296 | tf_op jit(solution)/shard_map/all_gather | solution.py:9
  1214.2 57.1 %all-gather.107.cloned.1.call-start = ((), (), s32[]{:S(2)}) async-start(), calls=%async_computation.25 | async-start | bytes 2359296 | tf_op jit(solution)/shard_map/all_gather | solution.py:9
  1215.0 91.9 %all-gather.109.cloned.1.call-start = ((), (), s32[]{:S(2)}) async-start(), calls=%async_computation.26 | async-start | bytes 2359296 | tf_op jit(solution)/shard_map/all_gather | solution.py:9
  1273.1 146.5 %all-gather.69.cloned.1.call-start = ((), (), s32[]{:S(2)}) async-start(), calls=%async_computation.6 | async-start | bytes 2621440 | tf_op jit(solution)/shard_map/all_gather | solution.py:9
  1373.5 77.4 %all-gather.111.cloned.1.call-start = ((), (), s32[]{:S(2)}) async-start(), calls=%async_computation.27 | async-start | bytes 2359296 | tf_op jit(solution)/shard_map/all_gather | solution.py:9
  1423.8 57.2 %all-gather.113.cloned.1.call-start = ((), (), s32[]{:S(2)}) async-start(), calls=%async_computation.28 | async-start | bytes 2359296 | tf_op jit(solution)/shard_map/all_gather | solution.py:9
  1424.6 92.0 %all-gather.115.cloned.1.call-start = ((), (), s32[]{:S(2)}) async-start(), calls=%async_computation.29 | async-start | bytes 2359296 | tf_op jit(solution)/shard_map/all_gather | solution.py:9
  1482.8 146.4 %all-gather.71.cloned.1.call-start = ((), (), s32[]{:S(2)}) async-start(), calls=%async_computation.7 | async-start | bytes 2621440 | tf_op jit(solution)/shard_map/all_gather | solution.py:9
  1583.0 77.3 %all-gather.117.cloned.1.call-start = ((), (), s32[]{:S(2)}) async-start(), calls=%async_computation.30 | async-start | bytes 2359296 | tf_op jit(solution)/shard_map/all_gather | solution.py:9
  1633.3 57.2 %all-gather.119.cloned.1.call-start = ((), (), s32[]{:S(2)}) async-start(), calls=%async_computation.31 | async-start | bytes 2359296 | tf_op jit(solution)/shard_map/all_gather | solution.py:9
Sparse Core Ops, SparseCore 0:
  12.5 30.8 all-gather.72
  109.6 45.9 all-gather.56
  159.8 26.8 all-gather.74
  188.5 28.1 all-gather.76
  226.3 28.1 all-gather.78
  321.3 45.9 all-gather.58
  371.6 26.9 all-gather.80
  400.4 28.1 all-gather.82
  438.2 28.1 all-gather.84
  533.2 45.9 all-gather.60
  583.5 26.9 all-gather.86
  612.2 28.1 all-gather.88
  650.0 28.1 all-gather.90
  745.0 45.9 all-gather.62
  795.2 26.9 all-gather.92
  823.9 28.1 all-gather.94
  859.5 28.1 all-gather.96
  954.5 45.9 all-gather.64
  1004.8 26.9 all-gather.98
  1033.5 28.1 all-gather.100
  1063.6 33.6 all-gather.102
  1164.1 45.9 all-gather.66
  1214.3 26.9 all-gather.104
  1243.1 28.1 all-gather.106
  1273.2 33.6 all-gather.108
  1373.6 45.9 all-gather.68
  1423.9 26.9 all-gather.110
  1452.8 28.1 all-gather.112
  1482.9 33.6 all-gather.114
  1583.2 45.9 all-gather.70
  1633.4 26.8 all-gather.116
  1662.3 28.1 all-gather.118
